TPU v7x, 32 devices: a whole 2x2x4 slice. The times are simulated.
32 devices in a mesh: dp: 8 (over z, y), mp: 4 (over x, core).
Axes of the slice: x: 2, y: 2, z: 4, core: 2. Of those that a mesh axis runs over, the one named last changes fastest.
Arguments:
- tokens: bfloat16 [8, 1024, 1280], P('dp', 'mp'), may hold values from -6 to 6
- sizes: float32 [8, 1024], P('dp'), may hold values from 1 to 8
- ln1_gain: float32 [1280], replicated, may hold values from 0.25 to 1.75
- qkv_weight: bfloat16 [3, 1280, 1280], P(None, 'dp', 'mp'), may hold values from -0.15625 to 0.15625
- proj_weight: bfloat16 [1280, 1280], P('mp', 'dp'), may hold values from -0.15625 to 0.15625
- ln2_gain: float32 [1280], replicated, may hold values from 0.25 to 1.75
- fc1_weight: bfloat16 [1280, 5120], P('dp', 'mp'), may hold values from -0.15625 to 0.15625
- fc1_bias: float32 [5120], P('mp'), may hold values from -3 to 3
- fc2_weight: bfloat16 [5120, 1280], P('mp', 'dp'), may hold values from -0.078125 to 0.078125
- pair_source: int32 [8, 16], P('dp'), may hold values from 0 to 1022, as said below
- pair_target: int32 [8, 16], P('dp'), may hold values from 1 to 1023, as said below
- kept_order: int32 [8, 1008], P('dp'), may hold values from 0 to 1023, as said below
Outputs:
- merged_out: bfloat16 [8, 1008, 1280], P('dp', 'mp')
Inputs may be any that keep to these rules, and one draw needn't show every extreme that they name: `pair_source`: in each image the 16 entries are distinct even token indices. `pair_target`: odd token indices; several sources may join the same target. `kept_order`: in each image every token index that is not in pair_source appears exactly once.
All inputs are finite; a program needn't handle non-finite values.
Results may differ from a plain program's by a relative error of at most 0.017.
Values may be sent and summed in bfloat16 or wider, within the bound.
A program may use at most 64 MiB of HBM per device.

v0:
```python
import math
import jax
import jax.numpy as jnp
from jax import lax
from jax.sharding import PartitionSpec as P

D = 1280
HEADS = 16


def layer_norm(values, gain):
    center = values - jnp.mean(values, axis=-1, keepdims=True)
    spread = jnp.mean(center * center, axis=-1, keepdims=True)
    return center * lax.rsqrt(spread + 1e-06) * gain


def merge_rows(total, order_rows, source_ids, target_ids):
    kept_rows = jnp.take_along_axis(total, order_rows[:, :, None], axis=1)
    source_rows = jnp.take_along_axis(total, source_ids[:, :, None], axis=1)
    joins = (order_rows[:, :, None] == target_ids[:, None, :]).astype(jnp.float32)
    return kept_rows + jnp.einsum(
        "icr,ird->icd", joins, source_rows, precision=lax.Precision.HIGHEST
    )


def shards(
    tokens,
    sizes,
    ln1_gain,
    qkv_weight,
    proj_weight,
    ln2_gain,
    fc1_weight,
    fc1_bias,
    fc2_weight,
    pair_source,
    pair_target,
    kept_order,
):
    images, own_tokens, width = tokens.shape
    length = sizes.shape[1]
    kept_total = kept_order.shape[1]
    devices_mp = lax.axis_size("mp")
    own_start = lax.axis_index("mp") * own_tokens
    head_size = D // HEADS
    base = tokens.astype(jnp.float32)
    normed = layer_norm(base, ln1_gain).astype(jnp.bfloat16)
    whole = lax.all_gather(normed, "mp", axis=1, tiled=True)
    local_width = qkv_weight.shape[2]
    columns = whole
    projected = jnp.einsum(
        "ind,cdf->cinf",
        columns,
        lax.all_gather(qkv_weight, "dp", axis=1, tiled=True),
        preferred_element_type=jnp.float32,
    ).astype(jnp.bfloat16)
    local_heads = local_width // head_size
    shaped = projected.reshape(3, images, length, local_heads, head_size)
    queries = shaped[0]
    keys_all = shaped[1]
    values_all = shaped[2]
    size_bias = jnp.log(sizes)[:, None, None, :]
    block = min(512, length)
    outputs = []
    for begin in range(0, length, block):
        scores = (
            jnp.einsum(
                "iqhe,ikhe->ihqk",
                queries[:, begin : begin + block],
                keys_all,
                preferred_element_type=jnp.float32,
            )
            / math.sqrt(head_size)
            + size_bias
        )
        weights = jax.nn.softmax(scores, axis=-1).astype(jnp.bfloat16)
        attended_block = jnp.einsum(
            "ihqk,ikhe->iqhe", weights, values_all, preferred_element_type=jnp.float32
        )
        outputs.append(attended_block.astype(jnp.bfloat16).reshape(images, block, local_width))
    attended = jnp.concatenate(outputs, axis=1)
    branch = jnp.einsum(
        "ind,de->ine",
        attended,
        lax.all_gather(proj_weight, "dp", axis=1, tiled=True),
        preferred_element_type=jnp.float32,
    )
    weighted = sizes[:, :, None] * branch
    own_sizes = lax.dynamic_slice_in_dim(sizes, own_start, own_tokens, 1)
    own_weighted = own_sizes[:, :, None] * base
    local_total = lax.dynamic_update_slice_in_dim(
        weighted,
        lax.dynamic_slice_in_dim(weighted, own_start, own_tokens, 1) + own_weighted,
        own_start,
        1,
    )
    merged_count = kept_total // devices_mp
    own_order = lax.dynamic_slice_in_dim(
        kept_order, lax.axis_index("mp") * merged_count, merged_count, 1
    )
    scattered = lax.psum_scatter(
        jnp.transpose(
            merge_rows(local_total, kept_order, pair_source, pair_target), (1, 0, 2)
        ).astype(jnp.bfloat16),
        "mp",
        scatter_dimension=0,
        tiled=True,
    ).astype(jnp.float32)
    numerator = jnp.transpose(scattered, (1, 0, 2))
    merged_size = merge_rows(sizes[:, :, None], own_order, pair_source, pair_target)
    merged = numerator / merged_size
    normed_two = layer_norm(merged, ln2_gain).astype(jnp.bfloat16)
    gathered = lax.all_gather(normed_two, "mp", axis=1, tiled=True)
    columns = gathered
    hidden_sum = jnp.einsum(
        "imd,df->imf",
        columns,
        lax.all_gather(fc1_weight, "dp", axis=0, tiled=True),
        preferred_element_type=jnp.float32,
    )
    hidden = jax.nn.gelu(hidden_sum + fc1_bias).astype(jnp.bfloat16)
    partial_out = jnp.einsum(
        "imf,fd->imd",
        hidden,
        lax.all_gather(fc2_weight, "dp", axis=1, tiled=True),
        preferred_element_type=jnp.float32,
    )
    mlp_part = lax.psum_scatter(
        partial_out.astype(jnp.bfloat16), "mp", scatter_dimension=1, tiled=True
    ).astype(jnp.float32)
    return (merged + mlp_part).astype(jnp.bfloat16)


def solution(mesh):
    return jax.shard_map(
        shards,
        mesh=mesh,
        in_specs=(
            P("dp", "mp", None),
            P("dp", None),
            P(),
            P(None, "dp", "mp"),
            P("mp", "dp"),
            P(),
            P("dp", "mp"),
            P("mp"),
            P("mp", "dp"),
            P("dp", None),
            P("dp", None),
            P("dp", None),
        ),
        out_specs=P("dp", "mp", None),
        check_vma=False,
    )
```

profile of v0, /device:TPU:1, one launch (start us, length us, event | category | flops | bytes accessed | tf_op | source)
XLA Modules:
  0.0 317.7 jit_solution(4380768634615341311)
XLA Ops:
  6.6 1.3 convert_reduce_fusion
  7.9 1.4 fusion.30
  9.3 2.2 fusion.32
  13.8 28.3 %all_gather.20 = bf16[320,1280]{0,1:T(8,128)(2,1)S(1)} all-gather(bf16[320,160]{0,1:T(8,128)(2,1)S(1)} %copy-done.2), channel_id=1, replica_groups=mesh['dp'=8,'mp'=4] {'dp'}, dimensions={1}, use_global_device_ids=true | all-gather | bytes 921600 | tf_op jit(solution)/shard_map/all_gather | solution.py:85
  42.8 1.4 gather_fusion.2
  44.4 53.4 %all-gather.8.cloned.1.call-done = bf16[3,1280,320]{2,1,0:T(8,128)(2,1)} async-done(((bf16[3,160,320]{2,1,0:T(8,128)(2,1)}), bf16[3,1280,320]{2,1,0:T(8,128)(2,1)}) %all-gather.8.cloned.1.call-update) | async-done | bytes 2457616 | tf_op jit(solution)/shard_map/all_gather | solution.py:54
  97.8 5.4 %convert_bitcast_fusion = bf16[3,1,1024,320]{2,3,0,1:T(8,128)(2,1)S(1)} fusion(bf16[3,1280,320]{2,1,0:T(8,128)(2,1)} %all-gather.8.cloned.1.call-done, bf16[1,1024,1280]{2,1,0:T(8,128)(2,1)} %all-gather.6.cloned.1.call-done), kind=kOutput, calls=%fused_computation.38 | convolution fusion | flops 2517565440 | bytes 7045120 | tf_op jit(solution)/shard_map/ind,cdf->cinf/dot_general | solution.py:51
  103.3 4.9 %fusion.80 = (f32[4,512]{1,0:T(4,128)S(1)}, f32[4,512,1024]{2,1,0:T(8,128)}) fusion(f32[1024]{0:T(1024)S(1)} %bitcast.179, bf16[1024,4,80]{0,2,1:T(8,128)(2,1)S(1)} %bitcast.170, bf16[1,1024,4,80]{1,3,2,0:T(8,128)(2,1)S(1)} %bitcast.168), kind=kOutput, calls=%fused_computation.120 | convolution fusion | flops 343933952 | bytes 9383936 | tf_op jit(solution)/shard_map/sub | solution.py:76
  108.2 4.9 %fusion.79 = (f32[4,512]{1,0:T(4,128)S(1)}, f32[4,512,1024]{2,1,0:T(8,128)}) fusion(f32[1024]{0:T(1024)S(1)} %bitcast.180, bf16[1024,4,80]{0,2,1:T(8,128)(2,1)S(1)} %bitcast.171, bf16[1,1024,4,80]{1,3,2,0:T(8,128)(2,1)S(1)} %bitcast.169), kind=kOutput, calls=%fused_computation.119 | convolution fusion | flops 343933952 | bytes 9383936 | tf_op jit(solution)/shard_map/sub | solution.py:76
  113.0 5.1 %fusion.37 = bf16[4,80,512]{2,1,0:T(8,128)(2,1)S(1)} fusion(bf16[1024,4,80]{0,2,1:T(8,128)(2,1)S(1)} %bitcast.166, f32[4,512,1024]{2,1,0:T(8,128)} %get-tuple-element.13, f32[4,512]{1,0:T(4,128)S(1)} %get-tuple-element.12), kind=kOutput, calls=%fused_computation.55 | convolution fusion | flops 339902464 | bytes 9379840 | tf_op jit(solution)/shard_map/ihqk,ikhe->iqhe/dot_general | solution.py:77
  118.9 1.7 fusion.36
  120.6 4.0 %convolution_multiply_fusion = f32[1024,1280]{1,0:T(8,128)} fusion(bf16[320,1280]{0,1:T(8,128)(2,1)S(1)} %all_gather.20, f32[1024]{0:T(1024)S(1)} %bitcast.165, bf16[1,512,320]{1,2,0:T(8,128)(2,1)S(1)} %bitcast.173, bf16[1,512,320]{1,2,0:T(8,128)(2,1)S(1)} %bitcast.172), kind=kOutput, calls=%fused_computation.24 | convolution fusion | flops 841482240 | bytes 6721536 | tf_op jit(solution)/shard_map/ind,de->ine/dot_general | solution.py:82
  124.6 1.4 constant_dynamic-slice_fusion.2
  127.3 3.1 gather_fusion.1
  130.5 9.7 %gather_fusion = f32[1008,1280]{1,0:T(8,128)} fusion(f32[1024,1280]{1,0:T(8,128)} %fusion.35, s32[1024]{0:T(1024)S(1)} %pad_clamp_fusion.2), kind=kCustom, calls=%fused_computation | custom fusion | bytes 10325952 | tf_op jit(solution)/shard_map/jit(take_along_axis)/gather | solution.py:18
  140.1 5.1 %fusion.21 = bf16[1008,1,1280]{2,0,1:T(8,128)(2,1)S(1)} fusion(f32[1008,1280]{1,0:T(8,128)} %gather_fusion, pred[1008]{0:T(1024)(128)(4,1)S(1)} %compare_and_fusion, f32[16,1280]{1,0:T(8,128)S(1)} %gather_fusion.1, pred[16]{0:T(512)(128)(4,1)S(1)} %compare_and_fusion.1, s32[1008]{0:T(1024)S(1)} %bitcast.175, s32[16]{0:T(128)S(1)} %bitcast.185), kind=kOutput, calls=%fused_computation.33 | convolution fusion | flops 251633408 | bytes 7828480 | tf_op jit(solution)/shard_map/icr,ird->icd/dot_general | solution.py:21
  145.2 27.6 %fusion = bf16[256,1280]{1,0:T(8,128)(2,1)S(1)} fusion(bf16[1008,1,1280]{2,0,1:T(8,128)(2,1)S(1)} %fusion.21), kind=kCustom, calls=%all-reduce-scatter | all-reduce-scatter fusion | flops 1310721 | bytes 3236352
  172.8 4.4 %collective-permute-start = (bf16[12,1280]{1,0:T(8,128)(2,1)S(1)}, bf16[12,1280]{1,0:T(8,128)(2,1)S(1)}, u32[]{:S(2)}, u32[]{:S(2)}) collective-permute-start(bf16[12,1280]{1,0:T(8,128)(2,1)S(1)} %slice.36), channel_id=1, source_target_pairs={{0,1},{1,2},{2,3},{4,5},{5,6},{6,7},{8,9},{9,10},{10,11},{12,13},{... | collective-permute-start | bytes 92168
  180.9 2.1 copy.14
  183.1 39.2 %all-gather.14.cloned.1.call-done = bf16[1280,1280]{0,1:T(8,128)(2,1)} async-done(((bf16[1280,160]{0,1:T(8,128)(2,1)}), bf16[1280,1280]{0,1:T(8,128)(2,1)}) %all-gather.14.cloned.1.call-update) | async-done | bytes 3276816 | tf_op jit(solution)/shard_map/all_gather | solution.py:125
  222.2 42.2 %all-gather.10.cloned.1.call-done = bf16[1,1008,1280]{2,0,1:T(2,128)(2,1)} async-done(((bf16[1,252,1280]{2,0,1:T(2,128)(2,1)}), bf16[1,1008,1280]{2,0,1:T(2,128)(2,1)}) %all-gather.10.cloned.1.call-update) | async-done | bytes 2580496 | tf_op jit(solution)/shard_map/all_gather | solution.py:113
  264.5 12.8 %fusion.20 = bf16[1,1008,1280]{2,1,0:T(8,128)(2,1)} fusion(bf16[1280,1280]{0,1:T(8,128)(2,1)} %all-gather.14.cloned.1.call-done, bf16[1280,1280]{1,0:T(8,128)(2,1)} %all-gather.12.cloned.1.call-done, bf16[1,1008,1280]{2,0,1:T(2,128)(2,1)} %all-gather.10.cloned.1.call-done, f32[1280]{0:T(1024)S(1)} %copy-done.7), kind=kOutput, calls=%fused_computation.32 | convolution fusion | flops 6620221440 | bytes 11719680 | tf_op jit(solution)/shard_map/imf,fd->imd/dot_general | solution.py:122
  277.3 26.0 %fusion.1 = bf16[256,1280]{1,0:T(8,128)(2,1)S(1)} fusion(bf16[1,1008,1280]{2,1,0:T(8,128)(2,1)} %fusion.20), kind=kCustom, calls=%all-reduce-scatter.1 | all-reduce-scatter fusion | flops 1310721 | bytes 3236352
  303.4 4.4 %collective-permute-start.1 = (bf16[12,1280]{1,0:T(8,128)(2,1)S(1)}, bf16[12,1280]{1,0:T(8,128)(2,1)S(1)}, u32[]{:S(2)}, u32[]{:S(2)}) collective-permute-start(bf16[12,1280]{1,0:T(8,128)(2,1)S(1)} %slice.37), channel_id=1, source_target_pairs={{0,1},{1,2},{2,3},{4,5},{5,6},{6,7},{8,9},{9,10},{10,11},{12,13},{... | collective-permute-start | bytes 92168
  (62 shorter events, 11.8 us)
Async XLA Ops:
  6.5 7.1 %copy-start.8 = (s32[1,16]{1,0:T(1,128)S(1)}, s32[1,16]{1,0:T(1,128)}, u32[]{:S(2)}) copy-start(s32[1,16]{1,0:T(1,128)} %param.21) | copy-start | bytes 196
  6.5 7.2 %copy-start = (f32[1,1024]{1,0:T(1,128)S(1)}, f32[1,1024]{1,0:T(1,128)}, u32[]{:S(2)}) copy-start(f32[1,1024]{1,0:T(1,128)} %param.13) | copy-start | bytes 12292
  6.5 7.2 %copy-start.2 = (bf16[320,160]{0,1:T(8,128)(2,1)S(1)}, bf16[320,160]{0,1:T(8,128)(2,1)}, u32[]{:S(2)}) copy-start(bf16[320,160]{0,1:T(8,128)(2,1)} %param.16) | copy-start | bytes 307204
  6.5 35.5 %copy-start.3 = (s32[1,1008]{1,0:T(1,128)S(1)}, s32[1,1008]{1,0:T(1,128)}, u32[]{:S(2)}) copy-start(s32[1,1008]{1,0:T(1,128)} %param.23) | copy-start | bytes 12100
  6.5 37.8 %all-gather.6.cloned.1.call-start = ((), (), s32[]{:S(2)}) async-start(), calls=%async_computation | async-start | bytes 3276800 | tf_op jit(solution)/shard_map/all_gather | solution.py:48
  7.9 36.3 %copy-start.5 = (s32[1,16]{1,0:T(1,128)S(1)}, s32[1,16]{1,0:T(1,128)}, u32[]{:S(2)}) copy-start(s32[1,16]{1,0:T(1,128)} %param.22) | copy-start | bytes 196
  11.6 86.2 %all-gather.8.cloned.1.call-start = ((), (), s32[]{:S(2)}) async-start(), calls=%async_computation.1 | async-start | bytes 3317760 | tf_op jit(solution)/shard_map/all_gather | solution.py:54
  12.3 170.7 %all-gather.12.cloned.1.call-start = ((), (), s32[]{:S(2)}) async-start(), calls=%async_computation.3 | async-start | bytes 3686400 | tf_op jit(solution)/shard_map/all_gather | solution.py:118
  13.0 209.2 %all-gather.14.cloned.1.call-start = ((), (), s32[]{:S(2)}) async-start(), calls=%async_computation.4 | async-start | bytes 3686400 | tf_op jit(solution)/shard_map/all_gather | solution.py:125
  13.6 250.8 %all-gather.10.cloned.1.call-start = ((), (), s32[]{:S(2)}) async-start(), calls=%async_computation.2 | async-start | bytes 6451200 | tf_op jit(solution)/shard_map/all_gather | solution.py:113
  113.0 5.9 %copy-start.9 = (f32[4,512,1024]{2,1,0:T(8,128)S(1)}, f32[4,512,1024]{2,1,0:T(8,128)}, u32[]{:S(2)}) copy-start(f32[4,512,1024]{2,1,0:T(8,128)} %get-tuple-element.11) | copy-start | bytes 25165828
  120.6 5.4 %copy-start.1 = (bf16[1,256,1280]{2,1,0:T(8,128)(2,1)S(1)}, bf16[1,256,1280]{2,1,0:T(8,128)(2,1)}, u32[]{:S(2)}) copy-start(bf16[1,256,1280]{2,1,0:T(8,128)(2,1)} %param.12) | copy-start | bytes 1966084
  145.2 32.0 %copy-start.6 = (u32[32]{0:T(128)S(1)}, u32[32]{0:T(128)}, u32[]{:S(2)}) copy-start(u32[32]{0:T(128)} %constant.99) | copy-start | bytes 388
  145.2 35.3 %copy-start.4 = (f32[1280]{0:T(1024)S(1)}, f32[1280]{0:T(1024)}, u32[]{:S(2)}) copy-start(f32[1280]{0:T(1024)} %param.17) | copy-start | bytes 15364
  172.8 5.7 %collective-permute-start = (bf16[12,1280]{1,0:T(8,128)(2,1)S(1)}, bf16[12,1280]{1,0:T(8,128)(2,1)S(1)}, u32[]{:S(2)}, u32[]{:S(2)}) collective-permute-start(bf16[12,1280]{1,0:T(8,128)(2,1)S(1)} %slice.36), channel_id=1, source_target_pairs={{0,1},{1,2},{2,3},{4,5},{5,6},{6,7},{8,9},{9,10},{10,11},{12,13},{... | collective-permute-start | bytes 92168
  179.6 84.9 %copy-start.7 = (f32[1280]{0:T(1024)S(1)}, f32[1280]{0:T(1024)}, u32[]{:S(2)}) copy-start(f32[1280]{0:T(1024)} %param.19) | copy-start | bytes 15364
  303.4 5.5 %collective-permute-start.1 = (bf16[12,1280]{1,0:T(8,128)(2,1)S(1)}, bf16[12,1280]{1,0:T(8,128)(2,1)S(1)}, u32[]{:S(2)}, u32[]{:S(2)}) collective-permute-start(bf16[12,1280]{1,0:T(8,128)(2,1)S(1)} %slice.37), channel_id=1, source_target_pairs={{0,1},{1,2},{2,3},{4,5},{5,6},{6,7},{8,9},{9,10},{10,11},{12,13},{... | collective-permute-start | bytes 92168
Sparse Core Ops, SparseCore 0:
  11.7 27.9 all-gather.5
  41.9 55.8 all-gather.7
  100.0 59.9 all-gather.11
  162.0 60.1 all-gather.13
  223.6 40.7 all-gather.9
where the time goes:
time: 318 us
  waiting for transfers between devices  138 us (43%)
  blocking collectives  81.9 us (26%)
  matrix products  44 us (14%)
  local copies, waits for them, and re-layouts  22 us (7%)
  between operations  14.1 us (4%)
  starting transfers between devices  8.96 us (3%)
  other arithmetic  8.93 us (3%)
    unnamed x2, blocking collectives  53.6 us
    all_gather x1, waiting for transfers between devices, shards(): lax.all_gather(qkv_weight, 'dp', axis=1, tiled=True)  53.4 us
    all_gather x1, waiting for transfers between devices, shards(): gathered = lax.all_gather(normed_two, 'mp', axis=1, tiled=True)  42.2 us
    all_gather x1, waiting for transfers between devices, shards(): lax.all_gather(fc2_weight, 'dp', axis=1, tiled=True)  39.2 us
    all_gather x1, blocking collectives, shards(): lax.all_gather(proj_weight, 'dp', axis=1, tiled=True)  28.3 us
    dot_general x1, matrix products, shards(): jnp.einsum('imf,fd->imd', hidden, lax.all_gather(fc2_weight, 'dp', axis=1...  12.8 us
    gather x2, local copies, waits for them, and re-layouts, merge_rows(): kept_rows = jnp.take_along_axis(total, order_rows[:, :, None], axis=1)  11 us
    sub x2, matrix products, shards(): weights = jax.nn.softmax(scores, axis=-1).astype(jnp.bfloat16)  9.7 us
  transfers between devices with their start and end apart: 7, of which 4 were waited for; matrix products, arithmetic and copies ran while one was open for 26% of the time, Pallas kernels for 0%

commit v1 on v0

--- a/solution.py
+++ b/solution.py
@@ -119,12 +119,19 @@
         preferred_element_type=jnp.float32,
     )
     hidden = jax.nn.gelu(hidden_sum + fc1_bias).astype(jnp.bfloat16)
-    partial_out = jnp.einsum(
-        "imf,fd->imd",
-        hidden,
-        lax.all_gather(fc2_weight, "dp", axis=1, tiled=True),
-        preferred_element_type=jnp.float32,
-    )
+    x = fc2_weight
+    ways, here, step = (lax.axis_size("dp"), lax.axis_index("dp"), x.shape[1])
+    results = []
+    for far in range(ways):
+        arriving = (
+            lax.ppermute(x, "dp", [(d, (d + 1) % ways) for d in range(ways)])
+            if far + 1 < ways
+            else x
+        )
+        results.append(jnp.einsum("imf,fd->imd", hidden, x, preferred_element_type=jnp.float32))
+        x = arriving
+    line = jnp.concatenate(results[::-1], axis=2)
+    partial_out = jnp.roll(line, (here + 1) * results[0].shape[2], axis=2)
     mlp_part = lax.psum_scatter(
         partial_out.astype(jnp.bfloat16), "mp", scatter_dimension=1, tiled=True
     ).astype(jnp.float32)

time: 318 us -> 339 us (1.066)
  local copies, waits for them, and re-layouts: 22 us -> 38.6 us
  matrix products: 44 us -> 51 us
  waiting for transfers between devices: 138 us -> 132 us
    ppermute x0 -> x7, waiting for transfers between devices: none -> 75.3 us  [shards(): lax.ppermute(x, 'dp', [(d, (d + 1) % ways) for d in range(ways)])]
    all_gather x1, waiting for transfers between devices: 42.2 us -> 0.01 us  [shards(): gathered = lax.all_gather(normed_two, 'mp', axis=1, tiled=True)]
    all_gather x1 -> x0, waiting for transfers between devices: 39.2 us -> none  [shards(): lax.all_gather(fc2_weight, 'dp', axis=1, tiled=True)]
    concatenate x0 -> x1, local copies, waits for them, and re-layouts: none -> 10.4 us  [shards(): partial_out = jnp.roll(line, (here + 1) * results[0].shape[2], axis=2)]
    dot_general x1 -> x9, matrix products: 12.8 us -> 19.9 us  [the longest x8 12.1 us: shards(): jnp.einsum('imf,fd->imd', hidden, x, preferred_element_type=jnp.float32)]
  transfers between devices with their start and end apart: 7 -> 13, of which waited for: 4 -> 8; matrix products, arithmetic and copies ran while one was open for 26% -> 29% of each run, Pallas kernels for 0% -> 0%
where the time goes in v1:
time: 339 us; the launch traced here: 338 us
  waiting for transfers between devices  132 us (39%)
  blocking collectives  84.2 us (25%)
  matrix products  51 us (15%)
  local copies, waits for them, and re-layouts  38.6 us (11%)
  between operations  14.2 us (4%)
  starting transfers between devices  9 us (3%)
  other arithmetic  8.91 us (3%)
    ppermute x7, waiting for transfers between devices, shards(): lax.ppermute(x, 'dp', [(d, (d + 1) % ways) for d in range(ways)])  75.3 us
    unnamed x2, blocking collectives  55.9 us
    all_gather x1, waiting for transfers between devices, shards(): lax.all_gather(qkv_weight, 'dp', axis=1, tiled=True)  54 us
    all_gather x1, blocking collectives, shards(): lax.all_gather(proj_weight, 'dp', axis=1, tiled=True)  28.3 us
    dot_general x8, matrix products, shards(): jnp.einsum('imf,fd->imd', hidden, x, preferred_element_type=jnp.float32)  12.1 us
    gather x2, local copies, waits for them, and re-layouts, merge_rows(): kept_rows = jnp.take_along_axis(total, order_rows[:, :, None], axis=1)  11.1 us
    concatenate x1, local copies, waits for them, and re-layouts, shards(): partial_out = jnp.roll(line, (here + 1) * results[0].shape[2], axis=2)  10.4 us
    sub x2, matrix products, shards(): weights = jax.nn.softmax(scores, axis=-1).astype(jnp.bfloat16)  9.67 us
  transfers between devices with their start and end apart: 13, of which 8 were waited for; matrix products, arithmetic and copies ran while one was open for 29% of the time, Pallas kernels for 0%

profile of v1, /device:TPU:1, one launch (start us, length us, event | category | flops | bytes accessed | tf_op | source)
XLA Modules:
  0.0 337.6 jit_solution(4954327375171128891)
XLA Ops:
  13.2 28.3 %all_gather.17 = bf16[320,1280]{0,1:T(8,128)(2,1)S(1)} all-gather(bf16[320,160]{0,1:T(8,128)(2,1)S(1)} %copy-done.2), channel_id=1, replica_groups=mesh['dp'=8,'mp'=4] {'dp'}, dimensions={1}, use_global_device_ids=true | all-gather | bytes 921600 | tf_op jit(solution)/shard_map/all_gather | solution.py:85
  43.8 54.0 %all-gather.7.cloned.1.call-done = bf16[3,1280,320]{2,1,0:T(8,128)(2,1)} async-done(((bf16[3,160,320]{2,1,0:T(8,128)(2,1)}), bf16[3,1280,320]{2,1,0:T(8,128)(2,1)}) %all-gather.7.cloned.1.call-update) | async-done | bytes 2457616 | tf_op jit(solution)/shard_map/all_gather | solution.py:54
  97.8 5.4 %convert_bitcast_fusion = bf16[3,1,1024,320]{2,3,0,1:T(8,128)(2,1)S(1)} fusion(bf16[3,1280,320]{2,1,0:T(8,128)(2,1)} %all-gather.7.cloned.1.call-done, bf16[1,1024,1280]{2,1,0:T(8,128)(2,1)} %all-gather.5.cloned.1.call-done), kind=kOutput, calls=%fused_computation.37 | convolution fusion | flops 2517565440 | bytes 7045120 | tf_op jit(solution)/shard_map/ind,cdf->cinf/dot_general | solution.py:51
  103.3 4.8 %fusion.73 = (f32[4,512]{1,0:T(4,128)S(1)}, f32[4,512,1024]{2,1,0:T(8,128)}) fusion(f32[1024]{0:T(1024)S(1)} %bitcast.206, bf16[1024,4,80]{0,2,1:T(8,128)(2,1)S(1)} %bitcast.197, bf16[1,1024,4,80]{1,3,2,0:T(8,128)(2,1)S(1)} %bitcast.195), kind=kOutput, calls=%fused_computation.123 | convolution fusion | flops 343933952 | bytes 9383936 | tf_op jit(solution)/shard_map/sub | solution.py:76
  108.1 4.8 %fusion.72 = (f32[4,512]{1,0:T(4,128)S(1)}, f32[4,512,1024]{2,1,0:T(8,128)}) fusion(f32[1024]{0:T(1024)S(1)} %bitcast.207, bf16[1024,4,80]{0,2,1:T(8,128)(2,1)S(1)} %bitcast.198, bf16[1,1024,4,80]{1,3,2,0:T(8,128)(2,1)S(1)} %bitcast.196), kind=kOutput, calls=%fused_computation.122 | convolution fusion | flops 343933952 | bytes 9383936 | tf_op jit(solution)/shard_map/sub | solution.py:76
  113.0 5.0 %fusion.36 = bf16[4,80,512]{2,1,0:T(8,128)(2,1)S(1)} fusion(bf16[1024,4,80]{0,2,1:T(8,128)(2,1)S(1)} %bitcast.193, f32[4,512,1024]{2,1,0:T(8,128)} %get-tuple-element.13, f32[4,512]{1,0:T(4,128)S(1)} %get-tuple-element.12), kind=kOutput, calls=%fused_computation.62 | convolution fusion | flops 339902464 | bytes 9379840 | tf_op jit(solution)/shard_map/ihqk,ikhe->iqhe/dot_general | solution.py:77
  120.6 4.0 %convolution_multiply_fusion = f32[1024,1280]{1,0:T(8,128)} fusion(bf16[320,1280]{0,1:T(8,128)(2,1)S(1)} %all_gather.17, f32[1024]{0:T(1024)S(1)} %bitcast.192, bf16[1,512,320]{1,2,0:T(8,128)(2,1)S(1)} %bitcast.200, bf16[1,512,320]{1,2,0:T(8,128)(2,1)S(1)} %bitcast.199), kind=kOutput, calls=%fused_computation.25 | convolution fusion | flops 841482240 | bytes 6721536 | tf_op jit(solution)/shard_map/ind,de->ine/dot_general | solution.py:82
  127.4 3.1 gather_fusion.1
  130.5 9.7 %gather_fusion = f32[1008,1280]{1,0:T(8,128)} fusion(f32[1024,1280]{1,0:T(8,128)} %fusion.34, s32[1024]{0:T(1024)S(1)} %pad_clamp_fusion.2), kind=kCustom, calls=%fused_computation | custom fusion | bytes 10325952 | tf_op jit(solution)/shard_map/jit(take_along_axis)/gather | solution.py:18
  140.2 5.1 %fusion.20 = bf16[1008,1,1280]{2,0,1:T(8,128)(2,1)S(1)} fusion(f32[1008,1280]{1,0:T(8,128)} %gather_fusion, pred[1008]{0:T(1024)(128)(4,1)S(1)} %compare_and_fusion, f32[16,1280]{1,0:T(8,128)S(1)} %gather_fusion.1, pred[16]{0:T(512)(128)(4,1)S(1)} %compare_and_fusion.1, s32[1008]{0:T(1024)S(1)} %bitcast.202, s32[16]{0:T(128)S(1)} %bitcast.212), kind=kOutput, calls=%fused_computation.32 | convolution fusion | flops 251633408 | bytes 7828480 | tf_op jit(solution)/shard_map/icr,ird->icd/dot_general | solution.py:21
  145.3 27.6 %fusion = bf16[256,1280]{1,0:T(8,128)(2,1)S(1)} fusion(bf16[1008,1,1280]{2,0,1:T(8,128)(2,1)S(1)} %fusion.20), kind=kCustom, calls=%all-reduce-scatter | all-reduce-scatter fusion | flops 1310721 | bytes 3236352
  172.9 4.4 %collective-permute-start.7 = (bf16[12,1280]{1,0:T(8,128)(2,1)S(1)}, bf16[12,1280]{1,0:T(8,128)(2,1)S(1)}, u32[]{:S(2)}, u32[]{:S(2)}) collective-permute-start(bf16[12,1280]{1,0:T(8,128)(2,1)S(1)} %slice.36), channel_id=1, source_target_pairs={{0,1},{1,2},{2,3},{4,5},{5,6},{6,7},{8,9},{9,10},{10,11},{12,13},{... | collective-permute-start | bytes 92168
  183.2 12.6 %collective-permute-done = bf16[1280,160]{0,1:T(8,128)(2,1)S(1)} collective-permute-done((bf16[1280,160]{0,1:T(8,128)(2,1)S(1)}, bf16[1280,160]{0,1:T(8,128)(2,1)S(1)}, u32[]{:S(2)}, u32[]{:S(2)}) %collective-permute-start) | collective-permute-done | bytes 409632 | tf_op jit(solution)/shard_map/ppermute | solution.py:127
  195.8 14.0 %collective-permute-done.1 = bf16[1280,160]{0,1:T(8,128)(2,1)S(1)} collective-permute-done((bf16[1280,160]{0,1:T(8,128)(2,1)S(1)}, bf16[1280,160]{0,1:T(8,128)(2,1)S(1)}, u32[]{:S(2)}, u32[]{:S(2)}) %collective-permute-start.1) | collective-permute-done | bytes 409632 | tf_op jit(solution)/shard_map/ppermute | solution.py:127
  209.9 13.3 %collective-permute-done.2 = bf16[1280,160]{0,1:T(8,128)(2,1)S(1)} collective-permute-done((bf16[1280,160]{0,1:T(8,128)(2,1)S(1)}, bf16[1280,160]{0,1:T(8,128)(2,1)S(1)}, u32[]{:S(2)}, u32[]{:S(2)}) %collective-permute-start.2) | collective-permute-done | bytes 409632 | tf_op jit(solution)/shard_map/ppermute | solution.py:127
  223.2 12.5 %collective-permute-done.3 = bf16[1280,160]{0,1:T(8,128)(2,1)S(1)} collective-permute-done((bf16[1280,160]{0,1:T(8,128)(2,1)S(1)}, bf16[1280,160]{0,1:T(8,128)(2,1)S(1)}, u32[]{:S(2)}, u32[]{:S(2)}) %collective-permute-start.3) | collective-permute-done | bytes 409632 | tf_op jit(solution)/shard_map/ppermute | solution.py:127
  235.7 11.7 %collective-permute-done.4 = bf16[1280,160]{0,1:T(8,128)(2,1)} collective-permute-done((bf16[1280,160]{0,1:T(8,128)(2,1)S(1)}, bf16[1280,160]{0,1:T(8,128)(2,1)}, u32[]{:S(2)}, u32[]{:S(2)}) %collective-permute-start.4) | collective-permute-done | bytes 409632 | tf_op jit(solution)/shard_map/ppermute | solution.py:127
  247.4 11.1 %collective-permute-done.5 = bf16[1280,160]{0,1:T(8,128)(2,1)} collective-permute-done((bf16[1280,160]{0,1:T(8,128)(2,1)}, bf16[1280,160]{0,1:T(8,128)(2,1)}, u32[]{:S(2)}, u32[]{:S(2)}) %collective-permute-start.5) | collective-permute-done | bytes 409632 | tf_op jit(solution)/shard_map/ppermute | solution.py:127
  258.5 7.8 %fusion.13 = bf16[1008,1280]{1,0:T(8,128)(2,1)S(1)} fusion(bf16[1280,1280]{1,0:T(8,128)(2,1)} %all-gather.11.cloned.1.call-done, bf16[1,1008,1280]{2,0,1:T(2,128)(2,1)} %all-gather.9.cloned.1.call-done, f32[1280]{0:T(1024)S(1)} %copy-done.14), kind=kOutput, calls=%fused_computation.22 | convolution fusion | flops 3315916800 | bytes 8442880 | tf_op jit(solution)/shard_map/imd,df->imf/dot_general | solution.py:115
  278.8 10.4 %concatenate.10 = bf16[1,1008,2560]{2,1,0:T(8,128)(2,1)} concatenate(bf16[1,1008,160]{2,1,0:T(8,128)(2,1)} %convolution_bitcast_fusion.7, bf16[1,1008,160]{2,1,0:T(8,128)(2,1)S(1)} %convolution_bitcast_fusion.6, bf16[1,1008,160]{2,1,0:T(8,128)(2,1)S(1)} %convolution_bitcast_fusion.5, bf16[1,1008,160]{2,1,0:T(8,128)(2,1)S(1)} %convolution_bitcast_fusion.4, ...), dimensions={2} | concatenate | bytes 10321920 | tf_op jit(solution)/shard_map/jit(_roll_dynamic)/concatenate | solution.py:134
  289.2 3.0 dynamic-slice_convert_fusion
  292.2 28.4 %fusion.1 = bf16[256,1280]{1,0:T(8,128)(2,1)} fusion(bf16[1,1008,1280]{2,1,0:T(8,128)(2,1)S(1)} %dynamic-slice_convert_fusion), kind=kCustom, calls=%all-reduce-scatter.1 | all-reduce-scatter fusion | flops 1310721 | bytes 3236352
  321.4 4.4 %collective-permute-start.8 = (bf16[12,1280]{1,0:T(8,128)(2,1)S(1)}, bf16[12,1280]{1,0:T(8,128)(2,1)S(1)}, u32[]{:S(2)}, u32[]{:S(2)}) collective-permute-start(bf16[12,1280]{1,0:T(8,128)(2,1)S(1)} %slice.37), channel_id=1, source_target_pairs={{0,1},{1,2},{2,3},{4,5},{5,6},{6,7},{8,9},{9,10},{10,11},{12,13},{... | collective-permute-start | bytes 92168
  326.8 3.0 concatenate.12
  (97 shorter events, 35.1 us)
Async XLA Ops:
  6.5 6.6 %copy-start.15 = (s32[1,16]{1,0:T(1,128)S(1)}, s32[1,16]{1,0:T(1,128)}, u32[]{:S(2)}) copy-start(s32[1,16]{1,0:T(1,128)} %param.21) | copy-start | bytes 196
  6.5 6.6 %copy-start = (f32[1,1024]{1,0:T(1,128)S(1)}, f32[1,1024]{1,0:T(1,128)}, u32[]{:S(2)}) copy-start(f32[1,1024]{1,0:T(1,128)} %param.13) | copy-start | bytes 12292
  6.5 6.6 %copy-start.2 = (bf16[320,160]{0,1:T(8,128)(2,1)S(1)}, bf16[320,160]{0,1:T(8,128)(2,1)}, u32[]{:S(2)}) copy-start(bf16[320,160]{0,1:T(8,128)(2,1)} %param.16) | copy-start | bytes 307204
  6.5 34.9 %copy-start.3 = (s32[1,1008]{1,0:T(1,128)S(1)}, s32[1,1008]{1,0:T(1,128)}, u32[]{:S(2)}) copy-start(s32[1,1008]{1,0:T(1,128)} %param.23) | copy-start | bytes 12100
  6.5 37.3 %all-gather.5.cloned.1.call-start = ((), (), s32[]{:S(2)}) async-start(), calls=%async_computation | async-start | bytes 3276800 | tf_op jit(solution)/shard_map/all_gather | solution.py:48
  9.3 34.3 %copy-start.5 = (s32[1,16]{1,0:T(1,128)S(1)}, s32[1,16]{1,0:T(1,128)}, u32[]{:S(2)}) copy-start(s32[1,16]{1,0:T(1,128)} %param.22) | copy-start | bytes 196
  11.6 86.2 %all-gather.7.cloned.1.call-start = ((), (), s32[]{:S(2)}) async-start(), calls=%async_computation.1 | async-start | bytes 3317760 | tf_op jit(solution)/shard_map/all_gather | solution.py:54
  12.3 246.1 %all-gather.11.cloned.1.call-start = ((), (), s32[]{:S(2)}) async-start(), calls=%async_computation.3 | async-start | bytes 3686400 | tf_op jit(solution)/shard_map/all_gather | solution.py:118
  13.1 245.4 %all-gather.9.cloned.1.call-start = ((), (), s32[]{:S(2)}) async-start(), calls=%async_computation.2 | async-start | bytes 6451200 | tf_op jit(solution)/shard_map/all_gather | solution.py:113
  145.3 32.0 %copy-start.6 = (u32[32]{0:T(128)S(1)}, u32[32]{0:T(128)}, u32[]{:S(2)}) copy-start(u32[32]{0:T(128)} %constant.126) | copy-start | bytes 388
  145.3 35.3 %copy-start.4 = (f32[1280]{0:T(1024)S(1)}, f32[1280]{0:T(1024)}, u32[]{:S(2)}) copy-start(f32[1280]{0:T(1024)} %param.17) | copy-start | bytes 15364
  172.9 5.7 %collective-permute-start.7 = (bf16[12,1280]{1,0:T(8,128)(2,1)S(1)}, bf16[12,1280]{1,0:T(8,128)(2,1)S(1)}, u32[]{:S(2)}, u32[]{:S(2)}) collective-permute-start(bf16[12,1280]{1,0:T(8,128)(2,1)S(1)} %slice.36), channel_id=1, source_target_pairs={{0,1},{1,2},{2,3},{4,5},{5,6},{6,7},{8,9},{9,10},{10,11},{12,13},{... | collective-permute-start | bytes 92168
  180.1 78.4 %copy-start.14 = (f32[1280]{0:T(1024)S(1)}, f32[1280]{0:T(1024)}, u32[]{:S(2)}) copy-start(f32[1280]{0:T(1024)} %param.19) | copy-start | bytes 15364
  183.1 12.7 %collective-permute-start = (bf16[1280,160]{0,1:T(8,128)(2,1)S(1)}, bf16[1280,160]{0,1:T(8,128)(2,1)S(1)}, u32[]{:S(2)}, u32[]{:S(2)}) collective-permute-start(bf16[1280,160]{0,1:T(8,128)(2,1)S(1)} %copy-done.7), channel_id=1, source_target_pairs={{0,4},{4,8},{8,12},{12,16},{16,20},{20,24},{24,28},{28,0},{1,5},{5... | collective-permute-start | bytes 1228808 | tf_op jit(solution)/shard_map/ppermute | solution.py:127
  195.8 62.6 %copy-start.8 = (bf16[1280,160]{0,1:T(8,128)(2,1)}, bf16[1280,160]{0,1:T(8,128)(2,1)S(1)}, u32[]{:S(2)}) copy-start(bf16[1280,160]{0,1:T(8,128)(2,1)S(1)} %collective-permute-done) | copy-start | bytes 1228804
  195.8 14.0 %collective-permute-start.1 = (bf16[1280,160]{0,1:T(8,128)(2,1)S(1)}, bf16[1280,160]{0,1:T(8,128)(2,1)S(1)}, u32[]{:S(2)}, u32[]{:S(2)}) collective-permute-start(bf16[1280,160]{0,1:T(8,128)(2,1)S(1)} %collective-permute-done), channel_id=1, source_target_pairs={{0,4},{4,8},{8,12},{12,16},{16,20},{20,24},{24,28},{28,0},{1,5},{5... | collective-permute-start | bytes 1228808 | tf_op jit(solution)/shard_map/ppermute | solution.py:127
  209.9 56.5 %copy-start.10 = (bf16[1280,160]{0,1:T(8,128)(2,1)}, bf16[1280,160]{0,1:T(8,128)(2,1)S(1)}, u32[]{:S(2)}) copy-start(bf16[1280,160]{0,1:T(8,128)(2,1)S(1)} %collective-permute-done.1) | copy-start | bytes 1228804
  209.9 13.3 %collective-permute-start.2 = (bf16[1280,160]{0,1:T(8,128)(2,1)S(1)}, bf16[1280,160]{0,1:T(8,128)(2,1)S(1)}, u32[]{:S(2)}, u32[]{:S(2)}) collective-permute-start(bf16[1280,160]{0,1:T(8,128)(2,1)S(1)} %collective-permute-done.1), channel_id=1, source_target_pairs={{0,4},{4,8},{8,12},{12,16},{16,20},{20,24},{24,28},{28,0},{1,5},{5... | collective-permute-start | bytes 1228808 | tf_op jit(solution)/shard_map/ppermute | solution.py:127
  223.2 43.1 %copy-start.12 = (bf16[1280,160]{0,1:T(8,128)(2,1)}, bf16[1280,160]{0,1:T(8,128)(2,1)S(1)}, u32[]{:S(2)}) copy-start(bf16[1280,160]{0,1:T(8,128)(2,1)S(1)} %collective-permute-done.2) | copy-start | bytes 1228804
  223.2 12.5 %collective-permute-start.3 = (bf16[1280,160]{0,1:T(8,128)(2,1)S(1)}, bf16[1280,160]{0,1:T(8,128)(2,1)S(1)}, u32[]{:S(2)}, u32[]{:S(2)}) collective-permute-start(bf16[1280,160]{0,1:T(8,128)(2,1)S(1)} %collective-permute-done.2), channel_id=1, source_target_pairs={{0,4},{4,8},{8,12},{12,16},{16,20},{20,24},{24,28},{28,0},{1,5},{5... | collective-permute-start | bytes 1228808 | tf_op jit(solution)/shard_map/ppermute | solution.py:127
  235.7 11.7 %collective-permute-start.4 = (bf16[1280,160]{0,1:T(8,128)(2,1)S(1)}, bf16[1280,160]{0,1:T(8,128)(2,1)}, u32[]{:S(2)}, u32[]{:S(2)}) collective-permute-start(bf16[1280,160]{0,1:T(8,128)(2,1)S(1)} %collective-permute-done.3), channel_id=1, source_target_pairs={{0,4},{4,8},{8,12},{12,16},{16,20},{20,24},{24,28},{28,0},{1,5},{5... | collective-permute-start | bytes 1228808 | tf_op jit(solution)/shard_map/ppermute | solution.py:127
  247.4 11.1 %collective-permute-start.5 = (bf16[1280,160]{0,1:T(8,128)(2,1)}, bf16[1280,160]{0,1:T(8,128)(2,1)}, u32[]{:S(2)}, u32[]{:S(2)}) collective-permute-start(bf16[1280,160]{0,1:T(8,128)(2,1)} %collective-permute-done.4), channel_id=1, source_target_pairs={{0,4},{4,8},{8,12},{12,16},{16,20},{20,24},{24,28},{28,0},{1,5},{5... | collective-permute-start | bytes 1228808 | tf_op jit(solution)/shard_map/ppermute | solution.py:127
  258.5 17.7 %collective-permute-start.6 = (bf16[1280,160]{0,1:T(8,128)(2,1)}, bf16[1280,160]{0,1:T(8,128)(2,1)}, u32[]{:S(2)}, u32[]{:S(2)}) collective-permute-start(bf16[1280,160]{0,1:T(8,128)(2,1)} %collective-permute-done.5), channel_id=1, source_target_pairs={{0,4},{4,8},{8,12},{12,16},{16,20},{20,24},{24,28},{28,0},{1,5},{5... | collective-permute-start | bytes 1228808 | tf_op jit(solution)/shard_map/ppermute | solution.py:127
  321.4 5.5 %collective-permute-start.8 = (bf16[12,1280]{1,0:T(8,128)(2,1)S(1)}, bf16[12,1280]{1,0:T(8,128)(2,1)S(1)}, u32[]{:S(2)}, u32[]{:S(2)}) collective-permute-start(bf16[12,1280]{1,0:T(8,128)(2,1)S(1)} %slice.37), channel_id=1, source_target_pairs={{0,1},{1,2},{2,3},{4,5},{5,6},{6,7},{8,9},{9,10},{10,11},{12,13},{... | collective-permute-start | bytes 92168
  (6 other events, 14.0 us)
Sparse Core Ops, SparseCore 0:
  11.7 27.9 all-gather.4
  41.9 55.8 all-gather.6
  100.0 59.9 all-gather.10
  183.2 39.2 all-gather.8
